TPU v7x, 32 devices: a whole 2x2x4 slice. The times are simulated.
32 devices in a mesh: row: 4 (over y, core), col: 8 (over z, x).
Axes of the slice: x: 2, y: 2, z: 4, core: 2. Of those that a mesh axis runs over, the one named last changes fastest.
Arguments:
- excitons: float32 [1024, 1024], P('row', 'col'), may hold values from -500 to 500
- valence_energy: float32 [1024], P('row'), may hold values from -3 to -1
- conduction_energy: float32 [1024], P('col'), may hold values from 1 to 3
- psi_valence: float32 [4096, 1024], P('row', 'col'), may hold values from -0.1875 to 0.1875
- psi_conduction: float32 [4096, 1024], P('col', 'row'), may hold values from -0.1875 to 0.1875
- screened: float32 [4096, 4096], P('row', 'col'), may hold values from -0.9 to 0.975, as said below
Outputs:
- next_vector: float32 [1024, 1024], P('row', 'col')
- coefficients: float32 [4], replicated
Inputs may be any that keep to these rules, and one draw needn't show every extreme that they name: symmetric: screened[p, p'] = screened[p', p].
All inputs are finite; a program needn't handle non-finite values.
Results may differ from a plain program's by a relative error of at most 0.0003.
Values sent between devices are 32-bit elements; how exact they have to be, the bound alone decides.
A program may use at most 64 MiB of HBM per device.

v0:
```python
import jax
import jax.numpy as jnp
from jax import lax
from jax.experimental import pallas as pl
from jax.experimental.pallas import tpu as pltpu
from jax.sharding import PartitionSpec as P

NV = 1024
NC = 1024
STEPS = 2


EPS = 1e-06


def shards(excitons, valence_energy, conduction_energy, psi_valence, psi_conduction, screened):
    high = lax.Precision.HIGHEST
    count = NV * NC
    energy_gap = conduction_energy[None, :] - valence_energy[:, None]
    total = lax.psum(jnp.sum(excitons * excitons), ("row", "col"))
    vector = excitons / jnp.sqrt(total / count + EPS)
    previous = jnp.zeros_like(vector)
    beta_prev = jnp.zeros((), jnp.float32)
    values = []
    for step in range(STEPS):
        panel_valence = lax.all_gather(psi_valence, "col", axis=1, tiled=True)
        panel_conduction = lax.all_gather(psi_conduction, "row", axis=1, tiled=True)
        full_rows = lax.all_gather(vector, "col", axis=1, tiled=True)
        image_block = jnp.dot(full_rows, panel_conduction.T, precision=high)
        image_columns = lax.all_gather(image_block, "row", axis=0, tiled=True)
        points = jnp.dot(panel_valence, image_columns, precision=high)
        weighted = points * screened
        back_valence = lax.psum_scatter(
            jnp.dot(panel_valence.T, weighted, precision=high),
            "row",
            scatter_dimension=0,
            tiled=True,
        )
        back_flipped = back_valence.T
        kernel_flipped = lax.psum_scatter(
            jnp.dot(panel_conduction.T, back_flipped, precision=high),
            "col",
            scatter_dimension=0,
            tiled=True,
        )
        image = energy_gap * vector - kernel_flipped.T
        cross, square, older = lax.psum(
            (jnp.sum(vector * image), jnp.sum(image * image), jnp.sum(previous * image)),
            ("row", "col"),
        )
        alpha = cross / count
        residual = image - alpha * vector - beta_prev * previous
        squared = (
            square / count - alpha * alpha - 2.0 * beta_prev * older / count + beta_prev * beta_prev
        )
        beta = jnp.sqrt(squared + EPS)
        previous = vector
        vector = residual / beta
        beta_prev = beta
        values.append(alpha)
        values.append(beta)
    return (vector, jnp.stack(values))


MESH = pl.DeviceIdType.MESH
NN = (((1,), (0,)), ((), ()))
NT = (((1,), (1,)), ((), ()))


def halves(value):
    hi = value.astype(jnp.bfloat16)
    return hi, (value - hi.astype(jnp.float32)).astype(jnp.bfloat16)


def dot3(a, b, dims):
    dot = lambda u, v: lax.dot_general(u, v, dims, preferred_element_type=jnp.float32)
    return dot(a[0], b[0]) + (dot(a[0], b[1]) + dot(a[1], b[0]))


def fused(
    R, C, count,
    x_ref, ve_ref, ce_ref, pv_ref, pc_ref, w_ref,
    out_ref, coef_ref,
    xl, pvl, pcl, il, cr, yr, xr, zr, bk, kb, sa, sb,
    pv3, pc3, xs, im, wt, acc, wtr, q1, gap,
    qz_s, qz_r, qx_s, qx_r, vz_s, vz_r, vx_s, vx_r,
    cy_s, cy_r, cc_s, cc_r, iy_s, iy_r, ic_s, ic_r,
    cr_s, cr_r, yr_s, yr_r, xr_s, xr_r, zr_s, zr_r,
    sa_s, sa_r, sb_s, sb_r,
):
    NY, NZ = R // 2, C // 2
    r, c = lax.axis_index("row"), lax.axis_index("col")
    y, k, z, h = r // 2, r % 2, c // 2, c % 2
    pending = []

    def copy(src, dst, ss, rs, dev):
        return pltpu.make_async_remote_copy(
            src_ref=src, dst_ref=dst, send_sem=ss, recv_sem=rs, device_id=dev, device_id_type=MESH
        )

    def send(src, dst, ss, rs, dev):
        op = copy(src, dst, ss, rs, dev)
        op.start()
        pending.append(op)

    def wait(dst, ss, rs):
        copy(dst, dst, ss, rs, (r, c)).wait_recv()

    zdev = lambda d: (r, ((z + d) % NZ) * 2 + h)
    zsrc = lambda d: ((z - d + NZ) % NZ) * 2 + h
    xpeer = (r, z * 2 + 1 - h)
    ydev = lambda d: (((y + d) % NY) * 2 + k, c)
    ysrc = lambda d: ((y - d + NY) % NY) * 2 + k
    kpeer = (y * 2 + 1 - k, c)
    near = [d for d in range(1, NZ) if d in (1, NZ - 1)] + [d for d in range(2, NZ - 1)]

    barrier = pltpu.get_barrier_semaphore()
    for d in range(1, C):
        pl.semaphore_signal(barrier, inc=1, device_id=(r, (c + d) % C), device_id_type=MESH)
    for d in range(1, R):
        pl.semaphore_signal(barrier, inc=1, device_id=((r + d) % R, c), device_id_type=MESH)
    pl.semaphore_wait(barrier, C + R - 2)

    def col_z(own, land, ss, rs):
        for d in near:
            send(own, land.at[c], ss.at[d], rs.at[d], zdev(d))

    def col_own(own, land, ss, rs):
        send(own, land.at[c], ss.at[0], rs.at[0], xpeer)

    def col_forward(d, land, zs, zr_, ss, rs):
        slot = land.at[zsrc(d)]
        wait(slot, zs.at[d], zr_.at[d])
        send(slot, slot, ss.at[d], rs.at[d], xpeer)

    def col_done(d, land, ss, rs):
        wait(land.at[((z - d + NZ) % NZ) * 2 + 1 - h], ss.at[d], rs.at[d])

    def row_start(own, land, ys, yr_, cs, cr_):
        for d in range(1, NY):
            send(own, land.at[r], ys.at[d], yr_.at[d], ydev(d))
        send(own, land.at[r], cs.at[0], cr_.at[0], kpeer)

    def row_forward(d, land, ys, yr_, cs, cr_):
        slot = land.at[ysrc(d)]
        wait(slot, ys.at[d], yr_.at[d])
        send(slot, slot, cs.at[d], cr_.at[d], kpeer)

    def row_done(d, land, cs, cr_):
        wait(land.at[((y - d + NY) % NY) * 2 + 1 - k], cs.at[d], cr_.at[d])

    def reduce_start(i, values):
        rows = [jnp.broadcast_to(v.reshape(1, 1), (1, 128)) for v in values]
        rows += [jnp.zeros((1, 128), jnp.float32)] * (8 - len(rows))
        sa[i, c] = jnp.concatenate(rows, axis=0)
        for d in range(1, C):
            send(sa.at[i, c], sa.at[i, c], sa_s.at[i, d], sa_r.at[i, d], (r, (c + d) % C))

    def reduce_middle(i):
        for d in range(1, C):
            wait(sa.at[i, (c - d + C) % C], sa_s.at[i, d], sa_r.at[i, d])
        sb[i, r] = jnp.sum(sa[i], axis=0)
        for d in range(1, R):
            send(sb.at[i, r], sb.at[i, r], sb_s.at[i, d], sb_r.at[i, d], ((r + d) % R, c))

    def reduce_end(i):
        for d in range(1, R):
            wait(sb.at[i, (r - d + R) % R], sb_s.at[i, d], sb_r.at[i, d])
        total = jnp.sum(sb[i], axis=0)
        return [total[j : j + 1, :] for j in range(3)]

    col_z(x_ref, xl.at[0], qz_s.at[0], qz_r.at[0])
    col_own(x_ref, xl.at[0], qx_s.at[0], qx_r.at[0])
    row_start(pc_ref, pcl, cy_s, cy_r, cc_s, cc_r)
    half = pv_ref.shape[0] // 2
    part_of = lambda j: pl.ds(j * half, half)
    for j in range(2):
        col_z(pv_ref.at[part_of(j)], pvl.at[j], vz_s.at[j], vz_r.at[j])
    start = x_ref[...]
    xl[0, c] = start
    reduce_start(0, [jnp.sum(start * start)])
    for d in near:
        col_forward(d, xl.at[0], qz_s.at[0], qz_r.at[0], qx_s.at[0], qx_r.at[0])
    for j in range(2):
        col_own(pv_ref.at[part_of(j)], pvl.at[j], vx_s.at[j], vx_r.at[j])
    reduce_middle(0)
    wtr[...] = w_ref[...].T
    ve = jnp.broadcast_to(ve_ref[...], (ce_ref.shape[1], ve_ref.shape[1])).T
    gap[...] = ce_ref[...] - ve
    for d in range(1, NY):
        row_forward(d, pcl, cy_s, cy_r, cc_s, cc_r)
    ncl = x_ref.shape[1]

    def put_pv(j, block_z, block_h, value):
        hi, lo = halves(value)
        col = pl.ds(pl.multiple_of(block_h * ncl, 128), ncl)
        pv3[0, block_z, part_of(j), col] = hi
        pv3[1, block_z, part_of(j), col] = lo

    def put_pc(block, value):
        hi, lo = halves(value)
        pc3[0, block] = hi
        pc3[1, block] = lo

    put_pc(r, pc_ref[...])
    for j in range(2):
        put_pv(j, z, h, pv_ref[part_of(j), :])
    for d in range(NY):
        row_done(d, pcl, cc_s, cc_r)
    for d in range(1, R):
        other = (r + d) % R
        put_pc(other, pcl[other])
    (total,) = reduce_end(0)[:1]
    scale = 1.0 / jnp.sqrt(total / count + EPS)
    q1[...] = start * scale
    for d in range(NZ):
        col_done(d, xl.at[0], qx_s.at[0], qx_r.at[0])

    points = pc_ref.shape[0]
    tile = points // 2
    betas = None
    for s in range(2):
        for zz in range(NZ):
            for hh in range(2):
                b = zz * 2 + hh
                if s == 0:
                    value = xl[0, b] * scale
                else:
                    value = (xl[1, b] - alpha * (xl[0, b] * scale)) / beta
                hi, lo = halves(value)
                xs[0, zz, :, hh * ncl : (hh + 1) * ncl] = hi
                xs[1, zz, :, hh * ncl : (hh + 1) * ncl] = lo
        total = None
        for zz in range(NZ):
            part = dot3((pc3[0, zz], pc3[1, zz]), (xs[0, zz], xs[1, zz]), NT)
            total = part if total is None else total + part
        il[s, r] = total
        row_start(il.at[s, r], il.at[s], iy_s.at[s], iy_r.at[s], ic_s.at[s], ic_r.at[s])
        if s == 0:
            for d in near:
                for j in range(2):
                    col_forward(d, pvl.at[j], vz_s.at[j], vz_r.at[j], vx_s.at[j], vx_r.at[j])
                    put_pv(j, (z - d + NZ) % NZ, h, pvl[j, zsrc(d)])
                if d == near[0]:
                    for e in range(1, NY):
                        row_forward(e, il.at[s], iy_s.at[s], iy_r.at[s], ic_s.at[s], ic_r.at[s])
            for d in [0] + near:
                for j in range(2):
                    col_done(d, pvl.at[j], vx_s.at[j], vx_r.at[j])
                    zz = (z - d + NZ) % NZ
                    put_pv(j, zz, 1 - h, pvl[j, zz * 2 + 1 - h])

        def chunk(b, first):
            im[0], im[1] = halves(il[s, b])

            def body(i, carry):
                rows = pl.ds(pl.multiple_of(i * tile, tile), tile)
                part = dot3((im[0, rows], im[1, rows]), (pv3[0, b], pv3[1, b]), NT)
                acc[rows, :] = part if first else acc[rows, :] + part
                return carry

            lax.fori_loop(0, points // tile, body, 0)

        chunk(r, True)
        row_done(0, il.at[s], ic_s.at[s], ic_r.at[s])
        chunk(y * 2 + 1 - k, False)
        for e in range(1, NY):
            if s == 1:
                row_forward(e, il.at[s], iy_s.at[s], iy_r.at[s], ic_s.at[s], ic_r.at[s])
            chunk(ysrc(e), False)
            row_done(e, il.at[s], ic_s.at[s], ic_r.at[s])
            chunk(((y - e + NY) % NY) * 2 + 1 - k, False)
        wt[0], wt[1] = halves(acc[...] * wtr[...])

        def back(b):
            def body(i, carry):
                rows = pl.ds(pl.multiple_of(i * tile, tile), tile)
                bk[s, b, rows, :] = dot3((wt[0, rows], wt[1, rows]), (pv3[0, b], pv3[1, b]), NN)
                return carry

            lax.fori_loop(0, points // tile, body, 0)

        for d in [*range(1, NY), 0]:
            mine, theirs = ((y + d) % NY) * 2 + k, ((y + d) % NY) * 2 + 1 - k
            back(theirs)
            send(bk.at[s, theirs], cr.at[s, d], cr_s.at[s, d], cr_r.at[s, d], kpeer)
            back(mine)
            wait(cr.at[s, d], cr_s.at[s, d], cr_r.at[s, d])
            bk[s, mine] = bk[s, mine] + cr[s, d]
            if d > 0:
                send(bk.at[s, mine], yr.at[s, d], yr_s.at[s, d], yr_r.at[s, d], ydev(d))
        summed = bk[s, r]
        for d in range(1, NY):
            wait(yr.at[s, d], yr_s.at[s, d], yr_r.at[s, d])
            summed = summed + yr[s, d]
        flat = halves(summed.T)
        far = [d for d in range(2, NZ - 1)] + [d for d in range(1, NZ) if d in (1, NZ - 1)] + [0]
        for d in far:
            zz = (z + d) % NZ
            part = dot3(flat, (pc3[0, zz], pc3[1, zz]), NN)
            kb[s, d, 0] = part[:, :ncl]
            kb[s, d, 1] = part[:, ncl:]
            send(kb.at[s, d, 1 - h], xr.at[s, d], xr_s.at[s, d], xr_r.at[s, d], xpeer)
        for d in far:
            wait(xr.at[s, d], xr_s.at[s, d], xr_r.at[s, d])
            kb[s, d, h] = kb[s, d, h] + xr[s, d]
            if d > 0:
                send(kb.at[s, d, h], zr.at[s, d], zr_s.at[s, d], zr_r.at[s, d], zdev(d))
        kernel = kb[s, 0, h]
        for d in near:
            wait(zr.at[s, d], zr_s.at[s, d], zr_r.at[s, d])
            kernel = kernel + zr[s, d]
        if s == 0:
            vector = q1[...]
            image = gap[...] * vector - kernel
            xl[1, c] = image
            col_z(xl.at[1, c], xl.at[1], qz_s.at[1], qz_r.at[1])
            col_own(xl.at[1, c], xl.at[1], qx_s.at[1], qx_r.at[1])
            reduce_start(1, [jnp.sum(vector * image), jnp.sum(image * image)])
            reduce_middle(1)
            for d in near:
                col_forward(d, xl.at[1], qz_s.at[1], qz_r.at[1], qx_s.at[1], qx_r.at[1])
            cross, square, _ = reduce_end(1)
            alpha = cross / count
            beta = jnp.sqrt(square / count - alpha * alpha + EPS)
            coef_ref[0:1, :] = alpha
            coef_ref[1:2, :] = beta
            for d in range(NZ):
                col_done(d, xl.at[1], qx_s.at[1], qx_r.at[1])
        else:
            vector = (xl[1, c] - alpha * q1[...]) / beta
            previous = q1[...]
            image = gap[...] * vector - kernel
            reduce_start(2, [jnp.sum(vector * image), jnp.sum(image * image), jnp.sum(previous * image)])
            reduce_middle(2)
            cross, square, older = reduce_end(2)
            alpha2 = cross / count
            squared = square / count - alpha2 * alpha2 - 2.0 * beta * older / count + beta * beta
            beta2 = jnp.sqrt(squared + EPS)
            out_ref[...] = (image - alpha2 * vector - beta * previous) / beta2
            coef_ref[2:3, :] = alpha2
            coef_ref[3:4, :] = beta2
    for op in pending:
        op.wait_send()


def fused_shards(R, C, excitons, valence_energy, conduction_energy, psi_valence, psi_conduction, screened):
    nv, nc = excitons.shape
    pr, pcn = screened.shape
    f32, bf16 = jnp.float32, jnp.bfloat16
    NY, NZ = R // 2, C // 2
    vm, dma = pltpu.VMEM, pltpu.SemaphoreType.DMA
    count = float(NV * NC)
    scratch = [
        vm((2, C, nv, nc), f32), vm((2, C, pr // 2, nc), f32), vm((R, pcn, nv), f32), vm((2, R, pcn, nv), f32),
        vm((2, NY, pcn, nv), f32), vm((2, NY, pcn, nv), f32),
        vm((2, NZ, nv, nc), f32), vm((2, NZ, nv, nc), f32),
        vm((2, R, pcn, nv), f32), vm((2, NZ, 2, nv, nc), f32),
        vm((3, C, 8, 128), f32), vm((3, R, 8, 128), f32),
        vm((2, R, pr, nv), bf16), vm((2, NZ, pcn, 2 * nc), bf16), vm((2, NZ, nv, 2 * nc), bf16),
        vm((2, pcn, nv), bf16), vm((2, pcn, pr), bf16), vm((pcn, pr), f32), vm((pcn, pr), f32),
        vm((nv, nc), f32), vm((nv, nc), f32),
    ]
    pairs = [(2, NZ), (2, NZ), (2, NZ), (2, NZ), (NY,), (NY,), (2, NY), (2, NY), (2, NY), (2, NY), (2, NZ), (2, NZ), (3, C), (3, R)]
    for shape in pairs:
        scratch += [dma(shape), dma(shape)]
    vector, coef = pl.pallas_call(
        lambda *refs: fused(R, C, count, *refs),
        out_shape=(jax.ShapeDtypeStruct((nv, nc), f32), jax.ShapeDtypeStruct((4, 128), f32)),
        in_specs=[pl.BlockSpec(memory_space=vm)] * 6,
        out_specs=(pl.BlockSpec(memory_space=vm), pl.BlockSpec(memory_space=vm)),
        scratch_shapes=scratch,
        compiler_params=pltpu.CompilerParams(collective_id=0, has_side_effects=True, vmem_limit_bytes=67043328),
    )(excitons, valence_energy.reshape(1, nv), conduction_energy.reshape(1, nc), psi_valence, psi_conduction, screened)
    return vector, coef[:, 0]


def solution(mesh):
    R, C = mesh.shape["row"], mesh.shape["col"]
    aligned = C == 2 * R and R % 2 == 0 and STEPS == 2 and NV == NC and (NV // R) % 128 == 0 and (NC // C) % 128 == 0
    body = (lambda *args: fused_shards(R, C, *args)) if aligned else shards
    return jax.shard_map(
        body,
        mesh=mesh,
        in_specs=(
            P("row", "col"),
            P("row"),
            P("col"),
            P("row", "col"),
            P("col", "row"),
            P("row", "col"),
        ),
        out_specs=(P("row", "col"), P()),
        check_vma=False,
    )
```

profile of v0, /device:TPU:0, one launch (start us, length us, event | category | flops | bytes accessed | tf_op | source)
XLA Modules:
  0.0 231.8 jit_solution(16141667440523974713)
XLA Ops:
  0.6 228.3 %shard_map.77 = (f32[256,128]{1,0:T(8,128)}, f32[4,128]{1,0:T(4,128)}) custom-call(f32[256,128]{1,0:T(8,128)} %refs_0_.1, f32[1,256]{1,0:T(1,128)} %bitcast.2, f32[1,128]{1,0:T(1,128)} %bitcast.3, f32[1024,128]{1,0:T(8,128)} %refs_3_.1, f32[512,256]{1,0:T(8,128)} %refs_4_.1, f32[1024,512]{1,0:T(8,128)} %refs_5_.1), custom_call_target="tpu_custom_call" | custom-call | tf_op jit(solution)/shard_map/pallas_call | solution.py:367
  229.0 1.3 slice_reduce_fusion
  230.3 1.6 copy.9
where the time goes:
time: 232 us
  Pallas kernels  228 us (98%)
  local copies, waits for them, and re-layouts  2.86 us (1%)
    pallas_call x1, Pallas kernels, fused_shards(): pl.pallas_call(lambda *refs: fused(R, C, count, *refs), out_shape=(jax.Sh...  228 us

commit v1 on v0

v1 whole, which is shorter than its diff:
```python
import jax
import jax.numpy as jnp
from jax import lax
from jax.experimental import pallas as pl
from jax.experimental.pallas import tpu as pltpu
from jax.sharding import PartitionSpec as P

NV = 1024
NC = 1024
STEPS = 2


EPS = 1e-06


def shards(excitons, valence_energy, conduction_energy, psi_valence, psi_conduction, screened):
    high = lax.Precision.HIGHEST
    count = NV * NC
    energy_gap = conduction_energy[None, :] - valence_energy[:, None]
    total = lax.psum(jnp.sum(excitons * excitons), ("row", "col"))
    vector = excitons / jnp.sqrt(total / count + EPS)
    previous = jnp.zeros_like(vector)
    beta_prev = jnp.zeros((), jnp.float32)
    values = []
    for step in range(STEPS):
        panel_valence = lax.all_gather(psi_valence, "col", axis=1, tiled=True)
        panel_conduction = lax.all_gather(psi_conduction, "row", axis=1, tiled=True)
        full_rows = lax.all_gather(vector, "col", axis=1, tiled=True)
        image_block = jnp.dot(full_rows, panel_conduction.T, precision=high)
        image_columns = lax.all_gather(image_block, "row", axis=0, tiled=True)
        points = jnp.dot(panel_valence, image_columns, precision=high)
        weighted = points * screened
        back_valence = lax.psum_scatter(
            jnp.dot(panel_valence.T, weighted, precision=high),
            "row",
            scatter_dimension=0,
            tiled=True,
        )
        back_flipped = back_valence.T
        kernel_flipped = lax.psum_scatter(
            jnp.dot(panel_conduction.T, back_flipped, precision=high),
            "col",
            scatter_dimension=0,
            tiled=True,
        )
        image = energy_gap * vector - kernel_flipped.T
        cross, square, older = lax.psum(
            (jnp.sum(vector * image), jnp.sum(image * image), jnp.sum(previous * image)),
            ("row", "col"),
        )
        alpha = cross / count
        residual = image - alpha * vector - beta_prev * previous
        squared = (
            square / count - alpha * alpha - 2.0 * beta_prev * older / count + beta_prev * beta_prev
        )
        beta = jnp.sqrt(squared + EPS)
        previous = vector
        vector = residual / beta
        beta_prev = beta
        values.append(alpha)
        values.append(beta)
    return (vector, jnp.stack(values))


MESH = pl.DeviceIdType.MESH
NN = (((1,), (0,)), ((), ()))
NT = (((1,), (1,)), ((), ()))
CHUNKS = 4
PIECES = 4
OPENING = (
    "t", "f0", "f1", "o2", "w3", "f2", "w2", "w1", "q", "o3", "a30", "c", "o1", "i",
    "x30", "a21", "a20", "a31", "x10", "a32", "a22", "s1", "a10", "j", "x21", "x22", "x20", "s0",
    "a11", "x32", "l", "a12", "x31", "x23", "x33", "p3", "g", "p2", "x11", "s2", "x12", "p0",
    "x13", "p1",
)
FIRST = (
    "b0", "b2", "s0", "b3", "b1", "s2", "s3", "k0", "s1", "k2", "z0", "z2", "h0", "k1",
    "k3", "h2", "z1", "f2", "z3", "h1", "f0", "m2", "h3", "r0", "f1", "m0", "e2", "f3",
    "m1", "a2", "m3", "e0", "e1", "a0", "a1", "e3", "a3",
)
SECOND = (
    "b2", "s2", "b0", "b3", "s0", "b1", "k2", "s1", "s3", "k0", "z2", "k1", "z0", "k3",
    "z1", "h0", "z3", "h1", "h2", "h3",
)


def halves(value):
    hi = value.astype(jnp.bfloat16)
    return hi, (value - hi.astype(jnp.float32)).astype(jnp.bfloat16)


def dot3(a, b, dims):
    dot = lambda u, v: lax.dot_general(u, v, dims, preferred_element_type=jnp.float32)
    return dot(a[0], b[0]) + (dot(a[0], b[1]) + dot(a[1], b[0]))


def fused(
    R, C, count,
    x_ref, ve_ref, ce_ref, pv_ref, pc_ref, w_ref,
    out_ref, coef_ref,
    ql, hl, pvl, pcl, il1, il2, bk, cr, yr, kb, xr, zr, sa, sb,
    pvt, pc3, xs, xh, it, wt, acc1, acc2, wtr, wv, q1, gap,
    w_s, qz_s, qz_r, qx_s, qx_r, vz_s, vz_r, vx_s, vx_r, cy_s, cy_r, cc_s, cc_r,
    jy_s, jy_r, jc_s, jc_r, iy_s, iy_r, ic_s, ic_r, gz_s, gz_r, gx_s, gx_r,
    cr_s, cr_r, yr_s, yr_r, xr_s, xr_r, zr_s, zr_r, sa_s, sa_r, sb_s, sb_r,
):
    NY, NZ = R // 2, C // 2
    r, c = lax.axis_index("row"), lax.axis_index("col")
    y, k, z, h = r // 2, r % 2, c // 2, c % 2
    nv, ncl = x_ref.shape
    np_, nvl = pv_ref.shape
    pcn, npc = pc_ref.shape
    m = nv // CHUNKS
    per = CHUNKS // 2
    pp = np_ // PIECES
    pending = []

    def copy(src, dst, ss, rs, dev):
        return pltpu.make_async_remote_copy(
            src_ref=src, dst_ref=dst, send_sem=ss, recv_sem=rs, device_id=dev, device_id_type=MESH
        )

    def send(src, dst, ss, rs, dev, when=None):
        args = (src, dst, ss, rs, dev)
        start = lambda: copy(*args).start()
        pl.when(when)(start) if when is not None else start()
        pending.append((when, args))

    def wait(dst, ss, rs):
        copy(dst, dst, ss, rs, (r, c)).wait_recv()

    zdev = lambda d: (r, ((z + d) % NZ) * 2 + h)
    zfrom = lambda d: (z - d + NZ) % NZ
    xpeer = (r, z * 2 + 1 - h)
    ydev = lambda d: (((y + d) % NY) * 2 + k, c)
    yfrom = lambda d: (y - d + NY) % NY
    kpeer = (y * 2 + 1 - k, c)
    near = [d for d in range(1, NZ) if d in (1, NZ - 1)] + [d for d in range(2, NZ - 1)]
    far = near[2:] + near[:2]

    load_w = pltpu.make_async_copy(w_ref, wv, w_s)
    load_w.start()
    barrier = pltpu.get_barrier_semaphore()
    for d in range(1, C):
        pl.semaphore_signal(barrier, inc=1, device_id=(r, (c + d) % C), device_id_type=MESH)
    for d in range(1, R):
        pl.semaphore_signal(barrier, inc=1, device_id=((r + d) % R, c), device_id_type=MESH)

    start = x_ref[...]
    ve = jnp.broadcast_to(ve_ref[...], (ncl, nv)).T
    gap[...] = ce_ref[...] - ve
    squares = start * start
    sums = [jnp.sum(squares), jnp.sum(squares * gap[...])]
    pl.semaphore_wait(barrier, C + R - 2)

    def reduce_start(i, values):
        rows = [jnp.broadcast_to(v.reshape(1, 1), (1, 128)) for v in values]
        rows += [jnp.zeros((1, 128), jnp.float32)] * (8 - len(rows))
        sa[i, c] = jnp.concatenate(rows, axis=0)
        for d in range(1, C):
            send(sa.at[i, c], sa.at[i, c], sa_s.at[i, d], sa_r.at[i, d], (r, (c + d) % C))

    def reduce_middle(i):
        for d in range(1, C):
            wait(sa.at[i, (c - d + C) % C], sa_s.at[i, d], sa_r.at[i, d])
        sb[i, r] = jnp.sum(sa[i], axis=0)
        for d in range(1, R):
            send(sb.at[i, r], sb.at[i, r], sb_s.at[i, d], sb_r.at[i, d], ((r + d) % R, c))

    def reduce_end(i):
        for d in range(1, R):
            wait(sb.at[i, (r - d + R) % R], sb_s.at[i, d], sb_r.at[i, d])
        total = jnp.sum(sb[i], axis=0)
        return [total[j : j + 1, 0:1] for j in range(3)]

    piece = lambda j: pl.ds(j * pp, pp)
    rows_of = lambda i: pl.ds(i * m, m)

    side = z // (NZ // 2)
    mirror = z + side * (NZ - 1 - 2 * z)

    def origin(n):
        o = n + (n + NZ - mirror) // NZ
        return o + side * (NZ - 1 - 2 * o)

    def zown(src, dst, ss, rs):
        for up in range(2):
            to = z + 2 * up - 1
            send(src, dst, ss.at[z, up], rs.at[z], (r, to * 2 + h), (to >= 0) & (to < NZ))

    def znext(o, slot, ss, rs):
        wait(slot, ss.at[o, 0], rs.at[o])
        up = (z - o - 1 + NZ) // NZ
        to = z + 2 * up - 1
        send(slot, slot, ss.at[o, 0], rs.at[o], (r, to * 2 + h), (to >= 0) & (to < NZ))

    def own_x(j):
        send(pv_ref.at[piece(j)], pvl.at[c, piece(j)], vx_s.at[j, z], vx_r.at[j, z], xpeer)

    def own_z(j):
        zown(pv_ref.at[piece(j)], pvl.at[c, piece(j)], vz_s.at[j, h], vz_r.at[j, h])

    zown(x_ref, ql.at[c], qz_s, qz_r)
    send(x_ref, ql.at[c], qx_s.at[z], qx_r.at[z], xpeer)
    for d in range(1, NY):
        send(pc_ref, pcl.at[r], cy_s.at[d], cy_r.at[d], ydev(d))
    send(pc_ref, pcl.at[r], cc_s.at[0], cc_r.at[0], kpeer)
    own_x(0)
    own_z(0)
    reduce_start(0, sums)

    def put_x(dst, t, rows, b, value):
        hi, lo = halves(value)
        dst[0, rows, b * ncl : (b + 1) * ncl] = hi
        dst[1, rows, b * ncl : (b + 1) * ncl] = lo

    def put_pc(b, value):
        hi, lo = halves(value)
        pc3[0, b] = hi
        pc3[1, b] = lo

    def put_pv(j, zz, hh, value):
        hi, lo = halves(value.T)
        for u in range(per):
            pvt[0, hh * per + u, zz, :, piece(j)] = hi[u * m : (u + 1) * m]
            pvt[1, hh * per + u, zz, :, piece(j)] = lo[u * m : (u + 1) * m]

    def first_rows(n):
        o = origin(n)
        slot = ql.at[o * 2 + h]
        znext(o, slot, qz_s, qz_r)
        send(slot, slot, qx_s.at[o], qx_r.at[o], xpeer)

    def shared_piece(n):
        o = origin(n)
        for hh in range(2):
            slot = pvl.at[o * 2 + hh, piece(0)]
            znext(o, slot, vz_s.at[0, hh], vz_r.at[0, hh])
            put_pv(0, o, hh, pvl[o * 2 + hh, piece(0), :])

    ql[c] = start
    put_pc(r, pc_ref[...])
    put_pv(0, z, h, pv_ref[piece(0), :])
    def image_of(ref, rows):
        total = None
        for b in range(R):
            cols = slice(b * npc, (b + 1) * npc)
            part = dot3((ref[0, rows, cols], ref[1, rows, cols]), (pc3[0, b], pc3[1, b]), NT)
            total = part if total is None else total + part
        return total

    def arrive(j, n):
        o = origin(n)
        slot = pvl.at[o * 2 + h, piece(j)]
        znext(o, slot, vz_s.at[j, h], vz_r.at[j, h])
        send(slot, slot, vx_s.at[j, o], vx_r.at[j, o], xpeer)
        put_pv(j, o, h, pvl[o * 2 + h, piece(j), :])

    def across(j, o):
        b = o * 2 + 1 - h
        wait(pvl.at[b, piece(j)], vx_s.at[j, o], vx_r.at[j, o])
        put_pv(j, o, 1 - h, pvl[b, piece(j), :])

    def points(j, scale):
        parts = [pvt[t, :, :, :, piece(j)].reshape(CHUNKS * R * m, pp) for t in range(2)]
        part = dot3((it[0], it[1]), parts, NN)
        acc1[:, piece(j)] = part
        wt[0, :, piece(j)], wt[1, :, piece(j)] = halves(part * scale * wtr[:, piece(j)])

    def flip(i, value):
        it[0, :, i * R * m : (i + 1) * R * m], it[1, :, i * R * m : (i + 1) * R * m] = halves(value.T)

    def first_image():
        for d in range(1, NY):
            slot = il1.at[yfrom(d) * 2 + k]
            wait(slot, jy_s.at[d], jy_r.at[d])
            send(slot, slot, jc_s.at[d], jc_r.at[d], kpeer)

    def flip_image():
        for d in range(NY):
            wait(il1.at[yfrom(d) * 2 + 1 - k], jc_s.at[d], jc_r.at[d])
        for i in range(CHUNKS):
            flip(i, jnp.concatenate([il1[b, rows_of(i), :] for b in range(R)], axis=0))

    def conduction():
        reduce_middle(0)
        wait(pcl.at[y * 2 + 1 - k], cc_s.at[0], cc_r.at[0])
        put_pc(y * 2 + 1 - k, pcl[y * 2 + 1 - k])
        for d in range(1, NY):
            slot = pcl.at[yfrom(d) * 2 + k]
            wait(slot, cy_s.at[d], cy_r.at[d])
            send(slot, slot, cc_s.at[d], cc_r.at[d], kpeer)
            put_pc(yfrom(d) * 2 + k, pcl[yfrom(d) * 2 + k])

    def send_image():
        for o in range(NZ):
            wait(ql.at[o * 2 + 1 - h], qx_s.at[o], qx_r.at[o])
        for b in range(C):
            put_x(xs, 0, slice(None), b, ql[b])
        for d in range(1, NY):
            b = yfrom(d) * 2 + 1 - k
            wait(pcl.at[b], cc_s.at[d], cc_r.at[d])
            put_pc(b, pcl[b])
        il1[r] = image_of(xs, slice(None))
        for d in range(1, NY):
            send(il1.at[r], il1.at[r], jy_s.at[d], jy_r.at[d], ydev(d))
        send(il1.at[r], il1.at[r], jc_s.at[0], jc_r.at[0], kpeer)

    def peer_piece():
        slot = pvl.at[z * 2 + 1 - h, piece(0)]
        wait(slot, vx_s.at[0, z], vx_r.at[0, z])
        zown(slot, slot, vz_s.at[0, 1 - h], vz_r.at[0, 1 - h])

    def peer_put():
        put_pv(0, z, 1 - h, pvl[z * 2 + 1 - h, piece(0), :])

    def flip_weights():
        load_w.wait()
        wtr[...] = wv[...].T

    def own_piece(j):
        own_z(j)
        put_pv(j, z, h, pv_ref[piece(j), :])

    def crossed(j, n):
        across(j, z if n == 0 else origin(n - 1))

    first = {}

    def normalise():
        total, gaps, _ = reduce_end(0)
        mean = total / count
        first["mean"] = mean
        first["scale"] = 1.0 / jnp.sqrt(mean + EPS)
        first["shift"] = (gaps / count) / (mean + EPS)

    def finish_piece(j):
        if not first:
            normalise()
        points(j, first["scale"])

    opening = dict(
        f=first_rows, q=peer_piece, g=peer_put, o=own_x, w=own_piece, s=shared_piece, a=arrive, x=crossed,
        t=flip_weights, c=conduction, i=send_image, j=first_image, l=flip_image, p=finish_piece,
    )
    for name in OPENING:
        opening[name[0]](*(int(v) for v in name[1:]))
    mean, scale, shift = first["mean"], first["scale"], first["shift"]
    q1[...] = start * scale
    gap[...] = gap[...] - shift

    zero = jnp.zeros((m, ncl), jnp.float32)
    sums = {0: [zero, zero], 1: [zero, zero, zero]}
    state = {}
    counts = [0, 0, 0]

    def back(s, i):
        lhs = [pvt[t, i].reshape(R * m, np_) for t in range(2)]
        part = dot3(lhs, (wt[0], wt[1]), NT)
        for b in range(R):
            bk[s, i, b % 2, b // 2] = part[b * m : (b + 1) * m]
        send(bk.at[s, i, 1 - k], cr.at[s, i], cr_s.at[s, i], cr_r.at[s, i], kpeer)

    def spread(s, i):
        wait(cr.at[s, i], cr_s.at[s, i], cr_r.at[s, i])
        for d in range(1, NY):
            yy = (y + d) % NY
            bk[s, i, k, yy] = bk[s, i, k, yy] + cr[s, i, yy]
            send(bk.at[s, i, k, yy], yr.at[s, i, d], yr_s.at[s, i, d], yr_r.at[s, i, d], ydev(d))

    def kernel_part(s, i):
        summed = bk[s, i, k, y] + cr[s, i, y]
        for d in range(1, NY):
            wait(yr.at[s, i, d], yr_s.at[s, i, d], yr_r.at[s, i, d])
            summed = summed + yr[s, i, d]
        flat = halves(summed)
        for b in range(R):
            part = dot3(flat, (pc3[0, b], pc3[1, b]), NN)
            for u in range(npc // ncl):
                at = b * (npc // ncl) + u
                kb[s, i, at % 2, at // 2] = part[:, u * ncl : (u + 1) * ncl]
        send(kb.at[s, i, 1 - h], xr.at[s, i], xr_s.at[s, i], xr_r.at[s, i], xpeer)

    def zsum(s, i):
        wait(xr.at[s, i], xr_s.at[s, i], xr_r.at[s, i])
        for d in far:
            zz = (z + d) % NZ
            kb[s, i, h, zz] = kb[s, i, h, zz] + xr[s, i, zz]
            send(kb.at[s, i, h, zz], zr.at[s, i, d], zr_s.at[s, i, d], zr_r.at[s, i, d], zdev(d))

    def vector_part(s, i):
        rows = rows_of(i)
        total = kb[s, i, h, z] + xr[s, i, z]
        for d in near:
            wait(zr.at[s, i, d], zr_s.at[s, i, d], zr_r.at[s, i, d])
            total = total + zr[s, i, d]
        before = q1[rows, :]
        if s == 0:
            image = gap[rows, :] * before - total
            hl[c, rows, :] = image
            own = hl.at[c, rows]
            for d in near:
                send(own, own, gz_s.at[i, d], gz_r.at[i, d], zdev(d))
            send(own, own, gx_s.at[i, 0], gx_r.at[i, 0], xpeer)
            sums[0][0] += before * image
            sums[0][1] += image * image
        else:
            vector = (hl[c, rows, :] - state["move"] * before) / state["beta"]
            image = gap[rows, :] * vector - total
            acc1[rows, :ncl] = vector
            acc1[rows, ncl : 2 * ncl] = image
            sums[1][0] += vector * image
            sums[1][1] += image * image
            sums[1][2] += before * image
        counts[s] += 1
        if counts[s] == CHUNKS:
            reduce_start(1 + s, [jnp.sum(v) for v in sums[s]])

    def forward(s, i):
        for d in near:
            slot = hl.at[zfrom(d) * 2 + h, rows_of(i)]
            wait(slot, gz_s.at[i, d], gz_r.at[i, d])
            send(slot, slot, gx_s.at[i, d], gx_r.at[i, d], xpeer)

    def image_part(s, i):
        rows = rows_of(i)
        for d in [0] + near:
            wait(hl.at[zfrom(d) * 2 + 1 - h, rows], gx_s.at[i, d], gx_r.at[i, d])
        for b in range(C):
            put_x(xh, 1, rows, b, hl[b, rows, :])
        il2[i, r] = image_of(xh, rows)
        own = il2.at[i, r]
        for d in range(1, NY):
            send(own, own, iy_s.at[i, d], iy_r.at[i, d], ydev(d))
        send(own, own, ic_s.at[i, 0], ic_r.at[i, 0], kpeer)

    def exchange(s, i):
        for d in range(1, NY):
            slot = il2.at[i, yfrom(d) * 2 + k]
            wait(slot, iy_s.at[i, d], iy_r.at[i, d])
            send(slot, slot, ic_s.at[i, d], ic_r.at[i, d], kpeer)

    def scalars(s, i):
        reduce_middle(1)

    def add_points(s, i):
        for d in range(NY):
            wait(il2.at[i, yfrom(d) * 2 + 1 - k], ic_s.at[i, d], ic_r.at[i, d])
        flip(i, il2[i].reshape(R * m, pcn))
        cols = slice(i * R * m, (i + 1) * R * m)
        counts[2] += 1
        last = counts[2] == CHUNKS
        if last:
            cross, square, _ = reduce_end(1)
            inside, norm = cross / count, mean / (mean + EPS)
            move = inside - shift * (EPS / (mean + EPS))
            beta = jnp.sqrt(square / count - 2.0 * move * inside + move * move * norm + EPS)
            state.update(move=move, beta=beta, norm=norm, alpha=shift + move)
            inverse, drop = 1.0 / beta, move * scale
        for j in range(PIECES):
            lanes = piece(j)
            rhs = [pvt[t, i, :, :, lanes].reshape(R * m, pp) for t in range(2)]
            part = dot3((it[0, :, cols], it[1, :, cols]), rhs, NN)
            if counts[2] > 1:
                part = acc2[:, lanes] + part
            if last:
                part = (part - drop * acc1[:, lanes]) * inverse * wtr[:, lanes]
                wt[0, :, lanes], wt[1, :, lanes] = halves(part)
            else:
                acc2[:, lanes] = part

    events = dict(
        b=back, s=spread, k=kernel_part, z=zsum, h=vector_part, f=forward,
        m=image_part, e=exchange, a=add_points, r=scalars,
    )
    for s, order in enumerate((FIRST, SECOND)):
        for name in order:
            events[name[0]](s, int(name[1:]))

    reduce_middle(2)
    cross, square, older = [v / count for v in reduce_end(2)]
    move, beta, norm, alpha = (state[n] for n in ("move", "beta", "norm", "alpha"))
    size = 1.0 - EPS / (beta * beta)
    overlap = (EPS / (mean + EPS)) * alpha / beta
    step = cross - shift * (EPS / (beta * beta))
    squared = (
        square + step * step * size + beta * beta * norm
        - 2.0 * step * cross - 2.0 * beta * older + 2.0 * step * beta * overlap
    )
    beta2 = jnp.sqrt(squared + EPS)
    vector, image = acc1[:nv, :ncl], acc1[:nv, ncl : 2 * ncl]
    out_ref[...] = (image - step * vector - beta * q1[...]) / beta2
    for j, value in enumerate((alpha, beta, shift + step, beta2)):
        coef_ref[j : j + 1, :] = jnp.broadcast_to(value, (1, 128))
    for when, args in pending:
        finish = lambda: copy(*args).wait_send()
        pl.when(when)(finish) if when is not None else finish()


def fused_shards(R, C, excitons, valence_energy, conduction_energy, psi_valence, psi_conduction, screened):
    nv, nc = excitons.shape
    pr, pcn = screened.shape
    nvl, npc = psi_valence.shape[1], psi_conduction.shape[1]
    f32, bf16 = jnp.float32, jnp.bfloat16
    NY, NZ = R // 2, C // 2
    n, m = CHUNKS, nv // CHUNKS
    vm, dma = pltpu.VMEM, pltpu.SemaphoreType.DMA
    count = float(NV * NC)
    scratch = [
        vm((C, nv, nc), f32), vm((C, nv, nc), f32), vm((C, pr, nvl), f32), vm((R, pcn, npc), f32),
        vm((R, nv, pcn), f32), vm((n, R, m, pcn), f32),
        vm((2, n, 2, NY, m, pcn), f32), vm((2, n, NY, m, pcn), f32), vm((2, n, NY, m, pcn), f32),
        vm((2, n, 2, NZ, m, nc), f32), vm((2, n, NZ, m, nc), f32), vm((2, n, NZ, m, nc), f32),
        vm((3, C, 8, 128), f32), vm((3, R, 8, 128), f32),
        vm((2, n, R, m, pr), bf16), vm((2, R, pcn, npc), bf16), vm((2, nv, NC), bf16), vm((2, nv, NC), bf16),
        vm((2, pcn, NV), bf16), vm((2, pcn, pr), bf16),
        vm((pcn, pr), f32), vm((pcn, pr), f32), vm((pcn, pr), f32), vm((pr, pcn), f32),
        vm((nv, nc), f32), vm((nv, nc), f32),
        dma(()),
    ]
    pairs = [
        [(NZ, 2), (NZ,)], (NZ,), [(PIECES, 2, NZ, 2), (PIECES, 2, NZ)], (PIECES, NZ), (NY,), (NY,), (NY,), (NY,), (n, NY), (n, NY), (n, NZ), (n, NZ),
        (2, n), (2, n, NY), (2, n), (2, n, NZ), (3, C), (3, R),
    ]
    for shape in pairs:
        both = shape if isinstance(shape, list) else [shape, shape]
        scratch += [dma(v) for v in both]
    vector, coef = pl.pallas_call(
        lambda *refs: fused(R, C, count, *refs),
        out_shape=(jax.ShapeDtypeStruct((nv, nc), f32), jax.ShapeDtypeStruct((4, 128), f32)),
        in_specs=[pl.BlockSpec(memory_space=vm)] * 5 + [pl.BlockSpec(memory_space=pl.ANY)],
        out_specs=(pl.BlockSpec(memory_space=vm), pl.BlockSpec(memory_space=vm)),
        scratch_shapes=scratch,
        compiler_params=pltpu.CompilerParams(collective_id=0, has_side_effects=True, vmem_limit_bytes=67043328),
    )(excitons, valence_energy.reshape(1, nv), conduction_energy.reshape(1, nc), psi_valence, psi_conduction, screened)
    return vector, coef[:, 0]


def solution(mesh):
    R, C = mesh.shape["row"], mesh.shape["col"]
    covered = max(int(v[1:]) for v in OPENING if v[0] == "f") == C // 2 - 2
    aligned = covered and C == 2 * R and R % 2 == 0 and STEPS == 2 and NV == NC and (NV // R) % (16 * CHUNKS) == 0 and (NV // R) % 128 == 0 and (NC // C) % 128 == 0
    body = (lambda *args: fused_shards(R, C, *args)) if aligned else shards
    return jax.shard_map(
        body,
        mesh=mesh,
        in_specs=(
            P("row", "col"),
            P("row"),
            P("col"),
            P("row", "col"),
            P("col", "row"),
            P("row", "col"),
        ),
        out_specs=(P("row", "col"), P()),
        check_vma=False,
    )
```

time: 232 us -> 156 us (0.67)
  Pallas kernels: 228 us -> 152 us
    pallas_call x1, Pallas kernels: 228 us -> 152 us  [fused_shards(): pl.pallas_call(lambda *refs: fused(R, C, count, *refs), out_shape=(jax.Sh...]
where the time goes in v1:
time: 156 us; the launch traced here: 155 us
  Pallas kernels  152 us (97%)
  local copies, waits for them, and re-layouts  2.86 us (2%)
    pallas_call x1, Pallas kernels, fused_shards(): pl.pallas_call(lambda *refs: fused(R, C, count, *refs), out_shape=(jax.Sh...  152 us

profile of v1, /device:TPU:0, one launch (start us, length us, event | category | flops | bytes accessed | tf_op | source)
XLA Modules:
  0.0 155.5 jit_solution(11768231151155286669)
XLA Ops:
  0.6 152.0 %shard_map.77 = (f32[256,128]{1,0:T(8,128)}, f32[4,128]{1,0:T(4,128)}) custom-call(f32[256,128]{1,0:T(8,128)} %refs_0_.1, f32[1,256]{1,0:T(1,128)} %bitcast.2, f32[1,128]{1,0:T(1,128)} %bitcast.3, f32[1024,128]{1,0:T(8,128)} %refs_3_.1, f32[512,256]{1,0:T(8,128)} %refs_4_.1, f32[1024,512]{1,0:T(8,128)} %refs_5_.1), custom_call_target="tpu_custom_call" | custom-call | tf_op jit(solution)/shard_map/pallas_call | solution.py:528
  152.6 1.3 slice_reduce_fusion
  153.9 1.6 %copy.9 = f32[256,128]{1,0:T(8,128)} copy(f32[256,128]{1,0:T(8,128)} %get-tuple-element.8) | data formatting | bytes 262144

commit v2 on v1

--- a/solution.py
+++ b/solution.py
@@ -65,7 +65,8 @@
 MESH = pl.DeviceIdType.MESH
 NN = (((1,), (0,)), ((), ()))
 NT = (((1,), (1,)), ((), ()))
-CHUNKS = 4
+CHUNKS = 8
+GROUP = 2
 PIECES = 4
 OPENING = (
     "t", "f0", "f1", "o2", "w3", "f2", "w2", "w1", "q", "o3", "a30", "c", "o1", "i",
@@ -74,13 +75,16 @@
     "x13", "p1",
 )
 FIRST = (
-    "b0", "b2", "s0", "b3", "b1", "s2", "s3", "k0", "s1", "k2", "z0", "z2", "h0", "k1",
-    "k3", "h2", "z1", "f2", "z3", "h1", "f0", "m2", "h3", "r0", "f1", "m0", "e2", "f3",
-    "m1", "a2", "m3", "e0", "e1", "a0", "a1", "e3", "a3",
+    "b3", "b0", "s7", "b1", "s6", "s2", "s0", "k7", "b2", "k6", "s1", "s4", "k2", "z7",
+    "k0", "z6", "k1", "z2", "s3", "k4", "s5", "z0", "h7", "z1", "z4", "k3", "k5", "h6",
+    "h0", "z5", "f7", "f6", "h4", "z3", "h2", "f0", "h1", "h5", "m6", "m7", "f4", "m0",
+    "f2", "h3", "f1", "m4", "f5", "m2", "e0", "e6", "f3", "m1", "e7", "r0", "m5", "m3",
+    "e1", "e2", "a3", "e4", "e5", "a0", "e3", "a2", "a1",
 )
 SECOND = (
-    "b2", "s2", "b0", "b3", "s0", "b1", "k2", "s1", "s3", "k0", "z2", "k1", "z0", "k3",
-    "z1", "h0", "z3", "h1", "h2", "h3",
+    "b0", "b1", "s0", "b3", "s3", "b2", "s2", "k0", "s7", "s6", "k3", "k2", "s1", "s4",
+    "s5", "z0", "k7", "z3", "k6", "z2", "k1", "z7", "k4", "z6", "k5", "z1", "z4", "z5",
+    "h6", "h1", "h0", "h3", "h4", "h2", "h7", "h5",
 )
 
 
@@ -98,11 +102,11 @@
     R, C, count,
     x_ref, ve_ref, ce_ref, pv_ref, pc_ref, w_ref,
     out_ref, coef_ref,
-    ql, hl, pvl, pcl, il1, il2, bk, cr, yr, kb, xr, zr, sa, sb,
+    ql, hl, pvl, pcl, il1, il2, bk, cr, yr, kb, xr, zr, sa, sb, sc,
     pvt, pc3, xs, xh, it, wt, acc1, acc2, wtr, wv, q1, gap,
     w_s, qz_s, qz_r, qx_s, qx_r, vz_s, vz_r, vx_s, vx_r, cy_s, cy_r, cc_s, cc_r,
     jy_s, jy_r, jc_s, jc_r, iy_s, iy_r, ic_s, ic_r, gz_s, gz_r, gx_s, gx_r,
-    cr_s, cr_r, yr_s, yr_r, xr_s, xr_r, zr_s, zr_r, sa_s, sa_r, sb_s, sb_r,
+    cr_s, cr_r, yr_s, yr_r, xr_s, xr_r, zr_s, zr_r, sa_s, sa_r, sb_s, sb_r, sc_s, sc_r,
 ):
     NY, NZ = R // 2, C // 2
     r, c = lax.axis_index("row"), lax.axis_index("col")
@@ -141,17 +145,16 @@
     load_w = pltpu.make_async_copy(w_ref, wv, w_s)
     load_w.start()
     barrier = pltpu.get_barrier_semaphore()
-    for d in range(1, C):
-        pl.semaphore_signal(barrier, inc=1, device_id=(r, (c + d) % C), device_id_type=MESH)
-    for d in range(1, R):
-        pl.semaphore_signal(barrier, inc=1, device_id=((r + d) % R, c), device_id_type=MESH)
+    for d in range(1, R * C):
+        at = (r * C + c + d) % (R * C)
+        pl.semaphore_signal(barrier, inc=1, device_id=(at // C, at % C), device_id_type=MESH)
 
     start = x_ref[...]
     ve = jnp.broadcast_to(ve_ref[...], (ncl, nv)).T
     gap[...] = ce_ref[...] - ve
     squares = start * start
     sums = [jnp.sum(squares), jnp.sum(squares * gap[...])]
-    pl.semaphore_wait(barrier, C + R - 2)
+    pl.semaphore_wait(barrier, R * C - 1)
 
     def reduce_start(i, values):
         rows = [jnp.broadcast_to(v.reshape(1, 1), (1, 128)) for v in values]
@@ -166,6 +169,25 @@
         sb[i, r] = jnp.sum(sa[i], axis=0)
         for d in range(1, R):
             send(sb.at[i, r], sb.at[i, r], sb_s.at[i, d], sb_r.at[i, d], ((r + d) % R, c))
+
+    others = range(1, R * C)
+
+    def place(d):
+        at = (r * C + c + d) % (R * C)
+        return at // C, at % C
+
+    def whole_start(values):
+        rows = [jnp.broadcast_to(v.reshape(1, 1), (1, 128)) for v in values]
+        rows += [jnp.zeros((1, 128), jnp.float32)] * (8 - len(rows))
+        sc[r * C + c] = jnp.concatenate(rows, axis=0)
+        for d in others:
+            send(sc.at[r * C + c], sc.at[r * C + c], sc_s.at[d], sc_r.at[d], place(d))
+
+    def whole_end():
+        for d in others:
+            wait(sc.at[(r * C + c + R * C - d) % (R * C)], sc_s.at[d], sc_r.at[d])
+        total = jnp.sum(sc[...], axis=0)
+        return [total[j : j + 1, 0:1] for j in range(3)]
 
     def reduce_end(i):
         for d in range(1, R):
@@ -354,12 +376,16 @@
     state = {}
     counts = [0, 0, 0]
 
-    def back(s, i):
-        lhs = [pvt[t, i].reshape(R * m, np_) for t in range(2)]
+    group = lambda g: range(g * GROUP, (g + 1) * GROUP)
+
+    def back(s, g):
+        lhs = [pvt[t, g * GROUP : (g + 1) * GROUP].reshape(GROUP * R * m, np_) for t in range(2)]
         part = dot3(lhs, (wt[0], wt[1]), NT)
-        for b in range(R):
-            bk[s, i, b % 2, b // 2] = part[b * m : (b + 1) * m]
-        send(bk.at[s, i, 1 - k], cr.at[s, i], cr_s.at[s, i], cr_r.at[s, i], kpeer)
+        for u, i in enumerate(group(g)):
+            for b in range(R):
+                at = (u * R + b) * m
+                bk[s, i, b % 2, b // 2] = part[at : at + m]
+            send(bk.at[s, i, 1 - k], cr.at[s, i], cr_s.at[s, i], cr_r.at[s, i], kpeer)
 
     def spread(s, i):
         wait(cr.at[s, i], cr_s.at[s, i], cr_r.at[s, i])
@@ -414,7 +440,8 @@
             sums[1][2] += before * image
         counts[s] += 1
         if counts[s] == CHUNKS:
-            reduce_start(1 + s, [jnp.sum(v) for v in sums[s]])
+            partial = [jnp.sum(v) for v in sums[s]]
+            reduce_start(1, partial) if s == 0 else whole_start(partial)
 
     def forward(s, i):
         for d in near:
@@ -443,13 +470,14 @@
     def scalars(s, i):
         reduce_middle(1)
 
-    def add_points(s, i):
-        for d in range(NY):
-            wait(il2.at[i, yfrom(d) * 2 + 1 - k], ic_s.at[i, d], ic_r.at[i, d])
-        flip(i, il2[i].reshape(R * m, pcn))
-        cols = slice(i * R * m, (i + 1) * R * m)
+    def add_points(s, g):
+        for i in group(g):
+            for d in range(NY):
+                wait(il2.at[i, yfrom(d) * 2 + 1 - k], ic_s.at[i, d], ic_r.at[i, d])
+            flip(i, il2[i].reshape(R * m, pcn))
+        cols = slice(g * GROUP * R * m, (g + 1) * GROUP * R * m)
         counts[2] += 1
-        last = counts[2] == CHUNKS
+        last = counts[2] == CHUNKS // GROUP
         if last:
             cross, square, _ = reduce_end(1)
             inside, norm = cross / count, mean / (mean + EPS)
@@ -459,7 +487,7 @@
             inverse, drop = 1.0 / beta, move * scale
         for j in range(PIECES):
             lanes = piece(j)
-            rhs = [pvt[t, i, :, :, lanes].reshape(R * m, pp) for t in range(2)]
+            rhs = [pvt[t, g * GROUP : (g + 1) * GROUP, :, :, lanes].reshape(GROUP * R * m, pp) for t in range(2)]
             part = dot3((it[0, :, cols], it[1, :, cols]), rhs, NN)
             if counts[2] > 1:
                 part = acc2[:, lanes] + part
@@ -477,8 +505,7 @@
         for name in order:
             events[name[0]](s, int(name[1:]))
 
-    reduce_middle(2)
-    cross, square, older = [v / count for v in reduce_end(2)]
+    cross, square, older = [v / count for v in whole_end()]
     move, beta, norm, alpha = (state[n] for n in ("move", "beta", "norm", "alpha"))
     size = 1.0 - EPS / (beta * beta)
     overlap = (EPS / (mean + EPS)) * alpha / beta
@@ -491,7 +518,7 @@
     vector, image = acc1[:nv, :ncl], acc1[:nv, ncl : 2 * ncl]
     out_ref[...] = (image - step * vector - beta * q1[...]) / beta2
     for j, value in enumerate((alpha, beta, shift + step, beta2)):
-        coef_ref[j : j + 1, :] = jnp.broadcast_to(value, (1, 128))
+        coef_ref[j] = value[0, 0]
     for when, args in pending:
         finish = lambda: copy(*args).wait_send()
         pl.when(when)(finish) if when is not None else finish()
@@ -511,7 +538,7 @@
         vm((R, nv, pcn), f32), vm((n, R, m, pcn), f32),
         vm((2, n, 2, NY, m, pcn), f32), vm((2, n, NY, m, pcn), f32), vm((2, n, NY, m, pcn), f32),
         vm((2, n, 2, NZ, m, nc), f32), vm((2, n, NZ, m, nc), f32), vm((2, n, NZ, m, nc), f32),
-        vm((3, C, 8, 128), f32), vm((3, R, 8, 128), f32),
+        vm((2, C, 8, 128), f32), vm((2, R, 8, 128), f32), vm((R * C, 8, 128), f32),
         vm((2, n, R, m, pr), bf16), vm((2, R, pcn, npc), bf16), vm((2, nv, NC), bf16), vm((2, nv, NC), bf16),
         vm((2, pcn, NV), bf16), vm((2, pcn, pr), bf16),
         vm((pcn, pr), f32), vm((pcn, pr), f32), vm((pcn, pr), f32), vm((pr, pcn), f32),
@@ -520,20 +547,20 @@
     ]
     pairs = [
         [(NZ, 2), (NZ,)], (NZ,), [(PIECES, 2, NZ, 2), (PIECES, 2, NZ)], (PIECES, NZ), (NY,), (NY,), (NY,), (NY,), (n, NY), (n, NY), (n, NZ), (n, NZ),
-        (2, n), (2, n, NY), (2, n), (2, n, NZ), (3, C), (3, R),
+        (2, n), (2, n, NY), (2, n), (2, n, NZ), (2, C), (2, R), (R * C,),
     ]
     for shape in pairs:
         both = shape if isinstance(shape, list) else [shape, shape]
         scratch += [dma(v) for v in both]
     vector, coef = pl.pallas_call(
         lambda *refs: fused(R, C, count, *refs),
-        out_shape=(jax.ShapeDtypeStruct((nv, nc), f32), jax.ShapeDtypeStruct((4, 128), f32)),
+        out_shape=(jax.ShapeDtypeStruct((nv, nc), f32), jax.ShapeDtypeStruct((4,), f32)),
         in_specs=[pl.BlockSpec(memory_space=vm)] * 5 + [pl.BlockSpec(memory_space=pl.ANY)],
-        out_specs=(pl.BlockSpec(memory_space=vm), pl.BlockSpec(memory_space=vm)),
+        out_specs=(pl.BlockSpec(memory_space=vm), pl.BlockSpec(memory_space=pltpu.SMEM)),
         scratch_shapes=scratch,
         compiler_params=pltpu.CompilerParams(collective_id=0, has_side_effects=True, vmem_limit_bytes=67043328),
     )(excitons, valence_energy.reshape(1, nv), conduction_energy.reshape(1, nc), psi_valence, psi_conduction, screened)
-    return vector, coef[:, 0]
+    return vector, coef
 
 
 def solution(mesh):

time: 156 us -> 149 us (0.955)
  Pallas kernels: 152 us -> 146 us
    pallas_call x1, Pallas kernels: 152 us -> 146 us  [fused_shards(): pl.pallas_call(lambda *refs: fused(R, C, count, *refs), out_shape=(jax.Sh...]
where the time goes in v2:
time: 149 us
  Pallas kernels  146 us (98%)
  local copies, waits for them, and re-layouts  2.74 us (2%)
    pallas_call x1, Pallas kernels, fused_shards(): pl.pallas_call(lambda *refs: fused(R, C, count, *refs), out_shape=(jax.Sh...  146 us

profile of v2, /device:TPU:0, one launch (start us, length us, event | category | flops | bytes accessed | tf_op | source)
XLA Modules:
  0.0 149.2 jit_solution(7730904898131504141)
XLA Ops:
  0.6 145.8 %shard_map.77 = (f32[256,128]{1,0:T(8,128)}, f32[4]{0:T(128)}) custom-call(f32[256,128]{1,0:T(8,128)} %refs_0_.1, f32[1,256]{1,0:T(1,128)} %bitcast.2, f32[1,128]{1,0:T(1,128)} %bitcast.3, f32[1024,128]{1,0:T(8,128)} %refs_3_.1, f32[512,256]{1,0:T(8,128)} %refs_4_.1, f32[1024,512]{1,0:T(8,128)} %refs_5_.1), custom_call_target="tpu_custom_call" | custom-call | tf_op jit(solution)/shard_map/pallas_call | solution.py:555
  146.5 1.6 %copy.10 = f32[256,128]{1,0:T(8,128)} copy(f32[256,128]{1,0:T(8,128)} %get-tuple-element.4) | data formatting | bytes 262144
  148.0 1.2 copy.11

commit v3 on v2

--- a/solution.py
+++ b/solution.py
@@ -69,10 +69,10 @@
 GROUP = 2
 PIECES = 4
 OPENING = (
-    "t", "f0", "f1", "o2", "w3", "f2", "w2", "w1", "q", "o3", "a30", "c", "o1", "i",
-    "x30", "a21", "a20", "a31", "x10", "a32", "a22", "s1", "a10", "j", "x21", "x22", "x20", "s0",
-    "a11", "x32", "l", "a12", "x31", "x23", "x33", "p3", "g", "p2", "x11", "s2", "x12", "p0",
-    "x13", "p1",
+    "o2", "t", "o3", "w3", "f0", "w2", "w1", "f1", "f2", "a10", "a21", "a20", "a12", "u",
+    "o1", "c", "a22", "i", "x20", "x22", "a11", "q", "a30", "s1", "j", "x23", "x21", "s0",
+    "a31", "g", "x11", "l", "x10", "x12", "a32", "x13", "x30", "p1", "p2", "x31", "s2", "x32",
+    "p0", "x33", "p3",
 )
 FIRST = (
     "b3", "b0", "s7", "b1", "s6", "s2", "s0", "k7", "b2", "k6", "s1", "s4", "k2", "z7",
@@ -100,11 +100,11 @@
 
 def fused(
     R, C, count,
-    x_ref, ve_ref, ce_ref, pv_ref, pc_ref, w_ref,
+    x_in, ve_in, ce_in, pv_in, pc_in, w_ref,
     out_ref, coef_ref,
     ql, hl, pvl, pcl, il1, il2, bk, cr, yr, kb, xr, zr, sa, sb, sc,
     pvt, pc3, xs, xh, it, wt, acc1, acc2, wtr, wv, q1, gap,
-    w_s, qz_s, qz_r, qx_s, qx_r, vz_s, vz_r, vx_s, vx_r, cy_s, cy_r, cc_s, cc_r,
+    x_ref, ve_ref, ce_ref, pv_ref, pc_ref, w_s, in_s, qz_s, qz_r, qx_s, qx_r, vz_s, vz_r, vx_s, vx_r, cy_s, cy_r, cc_s, cc_r,
     jy_s, jy_r, jc_s, jc_r, iy_s, iy_r, ic_s, ic_r, gz_s, gz_r, gx_s, gx_r,
     cr_s, cr_r, yr_s, yr_r, xr_s, xr_r, zr_s, zr_r, sa_s, sa_r, sb_s, sb_r, sc_s, sc_r,
 ):
@@ -142,18 +142,29 @@
     near = [d for d in range(1, NZ) if d in (1, NZ - 1)] + [d for d in range(2, NZ - 1)]
     far = near[2:] + near[:2]
 
+    loads = [
+        pltpu.make_async_copy(src, dst, in_s.at[j])
+        for j, (src, dst) in enumerate(
+            ((x_in, x_ref), (ve_in, ve_ref), (ce_in, ce_ref), (pv_in, pv_ref), (pc_in, pc_ref))
+        )
+    ]
     load_w = pltpu.make_async_copy(w_ref, wv, w_s)
-    load_w.start()
+    for load in loads + [load_w]:
+        load.start()
     barrier = pltpu.get_barrier_semaphore()
     for d in range(1, R * C):
         at = (r * C + c + d) % (R * C)
         pl.semaphore_signal(barrier, inc=1, device_id=(at // C, at % C), device_id_type=MESH)
 
+    for load in loads[:3]:
+        load.wait()
     start = x_ref[...]
     ve = jnp.broadcast_to(ve_ref[...], (ncl, nv)).T
     gap[...] = ce_ref[...] - ve
     squares = start * start
     sums = [jnp.sum(squares), jnp.sum(squares * gap[...])]
+    for load in loads[3:]:
+        load.wait()
     pl.semaphore_wait(barrier, R * C - 1)
 
     def reduce_start(i, values):
@@ -228,7 +239,6 @@
         send(pc_ref, pcl.at[r], cy_s.at[d], cy_r.at[d], ydev(d))
     send(pc_ref, pcl.at[r], cc_s.at[0], cc_r.at[0], kpeer)
     own_x(0)
-    own_z(0)
     reduce_start(0, sums)
 
     def put_x(dst, t, rows, b, value):
@@ -362,6 +372,7 @@
         points(j, first["scale"])
 
     opening = dict(
+        u=lambda: own_z(0),
         f=first_rows, q=peer_piece, g=peer_put, o=own_x, w=own_piece, s=shared_piece, a=arrive, x=crossed,
         t=flip_weights, c=conduction, i=send_image, j=first_image, l=flip_image, p=finish_piece,
     )
@@ -505,6 +516,12 @@
         for name in order:
             events[name[0]](s, int(name[1:]))
 
+    def settle(ops):
+        for when, args in ops:
+            finish = lambda: copy(*args).wait_send()
+            pl.when(when)(finish) if when is not None else finish()
+
+    settle(pending[: -len(others)])
     cross, square, older = [v / count for v in whole_end()]
     move, beta, norm, alpha = (state[n] for n in ("move", "beta", "norm", "alpha"))
     size = 1.0 - EPS / (beta * beta)
@@ -518,10 +535,14 @@
     vector, image = acc1[:nv, :ncl], acc1[:nv, ncl : 2 * ncl]
     out_ref[...] = (image - step * vector - beta * q1[...]) / beta2
     for j, value in enumerate((alpha, beta, shift + step, beta2)):
-        coef_ref[j] = value[0, 0]
-    for when, args in pending:
-        finish = lambda: copy(*args).wait_send()
-        pl.when(when)(finish) if when is not None else finish()
+        coef_ref[j : j + 1, :] = jnp.broadcast_to(value, (1, 128))
+    settle(pending[-len(others) :])
+
+
+def hand_over(vector_ref, coef_ref, out_ref, out_coef_ref):
+    out_ref[...] = vector_ref[...]
+    for j in range(4):
+        out_coef_ref[j] = coef_ref[j, 0]
 
 
 def fused_shards(R, C, excitons, valence_energy, conduction_energy, psi_valence, psi_conduction, screened):
@@ -543,7 +564,8 @@
         vm((2, pcn, NV), bf16), vm((2, pcn, pr), bf16),
         vm((pcn, pr), f32), vm((pcn, pr), f32), vm((pcn, pr), f32), vm((pr, pcn), f32),
         vm((nv, nc), f32), vm((nv, nc), f32),
-        dma(()),
+        vm((nv, nc), f32), vm((1, nv), f32), vm((1, nc), f32), vm((pr, nvl), f32), vm((pcn, npc), f32),
+        dma(()), dma((5,)),
     ]
     pairs = [
         [(NZ, 2), (NZ,)], (NZ,), [(PIECES, 2, NZ, 2), (PIECES, 2, NZ)], (PIECES, NZ), (NY,), (NY,), (NY,), (NY,), (n, NY), (n, NY), (n, NZ), (n, NZ),
@@ -554,13 +576,18 @@
         scratch += [dma(v) for v in both]
     vector, coef = pl.pallas_call(
         lambda *refs: fused(R, C, count, *refs),
-        out_shape=(jax.ShapeDtypeStruct((nv, nc), f32), jax.ShapeDtypeStruct((4,), f32)),
-        in_specs=[pl.BlockSpec(memory_space=vm)] * 5 + [pl.BlockSpec(memory_space=pl.ANY)],
-        out_specs=(pl.BlockSpec(memory_space=vm), pl.BlockSpec(memory_space=pltpu.SMEM)),
+        out_shape=(jax.ShapeDtypeStruct((nv, nc), f32), jax.ShapeDtypeStruct((8, 128), f32)),
+        in_specs=[pl.BlockSpec(memory_space=pl.ANY)] * 6,
+        out_specs=(pl.BlockSpec(memory_space=vm), pl.BlockSpec(memory_space=vm)),
         scratch_shapes=scratch,
         compiler_params=pltpu.CompilerParams(collective_id=0, has_side_effects=True, vmem_limit_bytes=67043328),
     )(excitons, valence_energy.reshape(1, nv), conduction_energy.reshape(1, nc), psi_valence, psi_conduction, screened)
-    return vector, coef
+    return pl.pallas_call(
+        hand_over,
+        out_shape=(jax.ShapeDtypeStruct((nv, nc), f32), jax.ShapeDtypeStruct((4,), f32)),
+        in_specs=[pl.BlockSpec(memory_space=vm)] * 2,
+        out_specs=(pl.BlockSpec(memory_space=vm), pl.BlockSpec(memory_space=pltpu.SMEM)),
+    )(vector, coef)
 
 
 def solution(mesh):

time: 149 us -> 147 us (0.987)
  local copies, waits for them, and re-layouts: 2.74 us -> 0 us
    unnamed x2 -> x0, local copies, waits for them, and re-layouts: 2.74 us -> none
    pallas_call x0 -> x1, Pallas kernels: none -> 1.58 us  [fused_shards(): pl.pallas_call(hand_over, out_shape=(jax.ShapeDtypeStruct((nv, nc), f32),...]
where the time goes in v3:
time: 147 us
  Pallas kernels  146 us (99%)
    pallas_call x1, Pallas kernels, fused_shards(): pl.pallas_call(lambda *refs: fused(R, C, count, *refs), out_shape=(jax.Sh...  145 us

profile of v3, /device:TPU:0, one launch (start us, length us, event | category | flops | bytes accessed | tf_op | source)
XLA Modules:
  0.0 146.9 jit_solution(9321004350961280795)
XLA Ops:
  0.6 144.5 %shard_map.77 = (f32[256,128]{1,0:T(8,128)}, f32[8,128]{1,0:T(8,128)}) custom-call(f32[256,128]{1,0:T(8,128)} %refs_0_.1, f32[1,256]{1,0:T(1,128)} %bitcast.2, f32[1,128]{1,0:T(1,128)} %bitcast.3, f32[1024,128]{1,0:T(8,128)} %refs_3_.1, f32[512,256]{1,0:T(8,128)} %refs_4_.1, f32[1024,512]{1,0:T(8,128)} %refs_5_.1), custom_call_target="tpu_custom_call" | custom-call | tf_op jit(solution)/shard_map/pallas_call | solution.py:577
  145.2 1.6 %shard_map.78 = (f32[256,128]{1,0:T(8,128)}, f32[4]{0:T(128)}) custom-call(f32[256,128]{1,0:T(8,128)} %get-tuple-element.4.vector_ref, f32[8,128]{1,0:T(8,128)} %get-tuple-element.5.coef_ref), custom_call_target="tpu_custom_call" | custom-call | tf_op jit(solution)/shard_map/pallas_call | solution.py:585

commit v4 on v3

--- a/solution.py
+++ b/solution.py
@@ -75,11 +75,11 @@
     "p0", "x33", "p3",
 )
 FIRST = (
-    "b3", "b0", "s7", "b1", "s6", "s2", "s0", "k7", "b2", "k6", "s1", "s4", "k2", "z7",
-    "k0", "z6", "k1", "z2", "s3", "k4", "s5", "z0", "h7", "z1", "z4", "k3", "k5", "h6",
-    "h0", "z5", "f7", "f6", "h4", "z3", "h2", "f0", "h1", "h5", "m6", "m7", "f4", "m0",
-    "f2", "h3", "f1", "m4", "f5", "m2", "e0", "e6", "f3", "m1", "e7", "r0", "m5", "m3",
-    "e1", "e2", "a3", "e4", "e5", "a0", "e3", "a2", "a1",
+    "b0", "b1", "s0", "s2", "b3", "s1", "b2", "k0", "s6", "s5", "k2", "s4", "s7", "s3",
+    "k1", "z0", "z2", "k6", "z1", "k4", "h0", "h2", "k3", "k5", "z4", "h1", "z3", "z5",
+    "z6", "k7", "f0", "f1", "h4", "h3", "f2", "z7", "h5", "m0", "h6", "f4", "m2", "f3",
+    "m1", "h7", "f5", "m4", "e2", "e0", "f6", "m3", "f7", "m5", "m6", "r0", "e3", "e4",
+    "m7", "e1", "a1", "e6", "e5", "a0", "e7", "a2", "a3",
 )
 SECOND = (
     "b0", "b1", "s0", "b3", "s3", "b2", "s2", "k0", "s7", "s6", "k3", "k2", "s1", "s4",

time: 147 us -> 149 us (1.014)
  Pallas kernels: 146 us -> 148 us
    pallas_call x1, Pallas kernels: 145 us -> 147 us  [fused_shards(): pl.pallas_call(lambda *refs: fused(R, C, count, *refs), out_shape=(jax.Sh...]
where the time goes in v4:
time: 149 us
  Pallas kernels  148 us (99%)
    pallas_call x1, Pallas kernels, fused_shards(): pl.pallas_call(lambda *refs: fused(R, C, count, *refs), out_shape=(jax.Sh...  147 us

profile of v4, /device:TPU:0, one launch (start us, length us, event | category | flops | bytes accessed | tf_op | source)
XLA Modules:
  0.0 149.0 jit_solution(18439073784622884645)
XLA Ops:
  0.6 146.6 %shard_map.77 = (f32[256,128]{1,0:T(8,128)}, f32[8,128]{1,0:T(8,128)}) custom-call(f32[256,128]{1,0:T(8,128)} %refs_0_.1, f32[1,256]{1,0:T(1,128)} %bitcast.2, f32[1,128]{1,0:T(1,128)} %bitcast.3, f32[1024,128]{1,0:T(8,128)} %refs_3_.1, f32[512,256]{1,0:T(8,128)} %refs_4_.1, f32[1024,512]{1,0:T(8,128)} %refs_5_.1), custom_call_target="tpu_custom_call" | custom-call | tf_op jit(solution)/shard_map/pallas_call | solution.py:577
  147.2 1.6 %shard_map.78 = (f32[256,128]{1,0:T(8,128)}, f32[4]{0:T(128)}) custom-call(f32[256,128]{1,0:T(8,128)} %get-tuple-element.4.vector_ref, f32[8,128]{1,0:T(8,128)} %get-tuple-element.5.coef_ref), custom_call_target="tpu_custom_call" | custom-call | tf_op jit(solution)/shard_map/pallas_call | solution.py:585
